TPU v7x, 32 devices: a whole 2x2x4 slice. The times are simulated.
32 devices in a mesh: row: 4 (over z), col: 8 (over y, x, core).
Axes of the slice: x: 2, y: 2, z: 4, core: 2. Of those that a mesh axis runs over, the one named last changes fastest.
Arguments:
- neighbor: int32 [32, 3072, 3072], P(None, 'col', 'row'), may hold values from 0 to 1, as said below
- true_coords: float32 [32, 3, 3072], P(None, None, ('row', 'col')), as said below
- pred_coords: float32 [32, 3, 3072], P(None, None, ('row', 'col')), as said below
- residue_mask: int32 [32, 3072], P(None, ('row', 'col')), may hold values from 0 to 1, as said below
- single: bfloat16 [32, 3072, 384], P(None, ('row', 'col'))
- ln_gain: float32 [384], replicated, may hold values from 0.1 to 1.9
- w_hidden: bfloat16 [384, 128], replicated, may hold values from -0.3125 to 0.3125
- b_hidden: float32 [128], replicated, may hold values from -3 to 3
- w_mid: bfloat16 [128, 128], replicated, may hold values from -0.5 to 0.5
- b_mid: float32 [128], replicated, may hold values from -3 to 3
- w_logits: bfloat16 [128, 50], replicated, may hold values from -1.5 to 1.5
- b_logits: float32 [50], replicated, may hold values from -4 to 4
Outputs:
- lddt_score: float32 [32, 3072], P(None, ('row', 'col'))
- residue_loss: float32 [32, 3072], P(None, ('row', 'col'))
- total_loss: float32 [], replicated
Inputs may be any that keep to these rules, and one draw needn't show every extreme that they name: `neighbor`: 0 or 1; 0 where j == i; 1 wherever 0 < |i - j| <= 8. `residue_mask`: per structure, 1 on a leading run of 1536 or more residues and 0 after it. `true_coords`: positions in angstroms. `pred_coords`: positions in angstroms.
All inputs are finite; a program needn't handle non-finite values.
Results may differ from a plain program's by a relative error of at most 0.00098.
Values sent between devices are 32-bit elements; how exact they have to be, the bound alone decides.
A program may use at most 128 MiB of HBM per device.

v0:
```python
import jax
import jax.numpy as jnp
from jax import lax
from jax.sharding import PartitionSpec as P

L = 3072
THRESHOLDS = (0.5, 1.0, 2.0, 4.0)


def from_root(shard, axis, root):
    mine = lax.axis_index(axis) == root
    return lax.psum(jnp.where(mine, shard, jnp.zeros_like(shard)), axis)


def tile_dist(rows_block, cols_block):
    total = (cols_block[:, 0, :, None] - rows_block[:, 0, None, :]) ** 2
    total = total + (cols_block[:, 1, :, None] - rows_block[:, 1, None, :]) ** 2
    total = total + (cols_block[:, 2, :, None] - rows_block[:, 2, None, :]) ** 2
    return jnp.sqrt(total + 1e-10)


def head_loss(lddt_value, single, ln_gain, w_hidden, b_hidden, w_mid, b_mid, w_logits, b_logits):
    features = single.astype(jnp.float32)
    average = jnp.mean(features, axis=-1, keepdims=True)
    centred = features - average
    variance = jnp.mean(centred * centred, axis=-1, keepdims=True)
    normed = (centred * lax.rsqrt(variance + 1e-05) * ln_gain).astype(jnp.bfloat16)
    first_hidden = jax.nn.relu(
        jnp.dot(normed, w_hidden, preferred_element_type=jnp.float32) + b_hidden
    ).astype(jnp.bfloat16)
    second_hidden = jax.nn.relu(
        jnp.dot(first_hidden, w_mid, preferred_element_type=jnp.float32) + b_mid
    ).astype(jnp.bfloat16)
    logits = jnp.dot(second_hidden, w_logits, preferred_element_type=jnp.float32) + b_logits
    log_total = jnp.log(jnp.sum(jnp.exp(logits), axis=-1))
    bins = logits.shape[-1]
    centers = (jnp.arange(bins).astype(jnp.float32) + 0.5) / bins
    closeness = jnp.exp(-((lddt_value[..., None] - centers) ** 2) * (bins * bins * 0.5))
    target = closeness / jnp.sum(closeness, axis=-1, keepdims=True)
    return log_total - jnp.sum(target * logits, axis=-1)


def local(
    neighbor,
    true_coords,
    pred_coords,
    residue_mask,
    single,
    ln_gain,
    w_hidden,
    b_hidden,
    w_mid,
    b_mid,
    w_logits,
    b_logits,
):
    valid = residue_mask.astype(jnp.float32)
    own_len = residue_mask.shape[1]
    stacked = jnp.concatenate([true_coords, pred_coords, valid[:, None, :]], axis=1)
    row_count = lax.axis_size("row")
    col_count = lax.axis_size("col")
    rows_len = L // row_count
    cols_len = L // col_count
    col_index = lax.axis_index("col")
    rows_part = lax.all_gather(stacked, "col", axis=2, tiled=True)
    offset = col_index * cols_len % rows_len
    column_piece = lax.dynamic_slice_in_dim(rows_part, offset, cols_len, 2)
    source_row = col_index * cols_len // rows_len
    cols_part = from_root(column_piece, "row", source_row)
    true_dist = tile_dist(rows_part[:, 0:3], cols_part[:, 0:3])
    pred_dist = tile_dist(rows_part[:, 3:6], cols_part[:, 3:6])
    mismatch = jnp.abs(pred_dist - true_dist)
    scores = jnp.zeros_like(mismatch)
    for threshold in THRESHOLDS:
        scores = scores + jax.nn.sigmoid(4.0 * (threshold - mismatch))
    scores = 0.25 * scores
    weights = neighbor.astype(jnp.float32) * rows_part[:, 6, None, :] * cols_part[:, 6, :, None]
    preserved = jnp.sum(weights * scores, axis=1)
    neighbors = jnp.sum(weights, axis=1)
    preserved_all, neighbors_all = lax.psum((preserved, neighbors), "col")
    preserved_own = lax.dynamic_slice_in_dim(preserved_all, col_index * own_len, own_len, 1)
    neighbors_own = lax.dynamic_slice_in_dim(neighbors_all, col_index * own_len, own_len, 1)
    lddt_score = preserved_own / jnp.maximum(neighbors_own, 1.0)
    residue_loss = valid * head_loss(
        lddt_score, single, ln_gain, w_hidden, b_hidden, w_mid, b_mid, w_logits, b_logits
    )
    loss_sum, valid_sum = lax.psum((jnp.sum(residue_loss), jnp.sum(valid)), ("row", "col"))
    total_loss = loss_sum / valid_sum
    return (lddt_score, residue_loss, total_loss)


def solution(mesh):
    placed = (
        P(None, "col", "row"),
        P(None, None, ("row", "col")),
        P(None, None, ("row", "col")),
        P(None, ("row", "col")),
        P(None, ("row", "col"), None),
        P(),
        P(),
        P(),
        P(),
        P(),
        P(),
        P(),
    )
    return jax.shard_map(
        local,
        mesh=mesh,
        in_specs=placed,
        out_specs=(P(None, ("row", "col")), P(None, ("row", "col")), P()),
        check_vma=False,
    )
```

profile of v0, /device:TPU:0, one launch (start us, length us, event | category | flops | bytes accessed | tf_op | source)
XLA Modules:
  0.0 312.7 jit_solution(15335422747212448188)
XLA Ops:
  7.2 0.0 copy-start
  7.2 0.0 all-reduce.5.cloned.1.call-start
  7.3 0.7 convert_bitcast_fusion
  8.0 0.8 pad_maximum_fusion
  8.8 0.9 copy.33
  9.7 21.3 %all_gather.3 = f32[32,7,768]{0,1,2:T(8,128)S(1)} all-gather(f32[32,7,96]{0,1,2:T(8,128)} %copy.33), channel_id=1, replica_groups=mesh['row'=4,'col'=8] {'col'}, dimensions={2}, use_global_device_ids=true | all-gather | bytes 774144 | tf_op jit(solution)/shard_map/all_gather | solution.py:65
  31.0 1.3 dynamic-slice_select_fusion
  32.3 0.0 all-reduce.5.cloned.1.call-update
  32.3 0.0 all-reduce.7.cloned.1.call-start
  32.4 3.3 %fusion.31 = (f32[32,1,768]{0,1,2:T(1,128)}, f32[32,1,768]{0,1,2:T(1,128)}, f32[32,1,768]{0,1,2:T(1,128)}, f32[32,1,768]{0,1,2:T(1,128)}, f32[32,1,768]{0,1,2:T(...) fusion(f32[32,7,768]{0,1,2:T(8,128)S(1)} %all_gather.3), kind=kLoop, calls=%fused_computation.43 | loop fusion | bytes 1376256 | tf_op jit(solution)/shard_map/slice | solution.py:77
  35.6 2.3 convert_reduce_fusion
  37.9 2.8 fusion.4
  40.8 0.0 copy-done
  40.8 3.2 %maximum_convert_fusion = bf16[32,96,128]{2,1,0:T(8,128)(2,1)S(1)} fusion(bf16[32,96,384]{2,1,0:T(8,128)(2,1)} %param.16, f32[384]{0:T(512)} %param.17, f32[32,96]{1,0:T(8,128)S(1)} %add_rsqrt_fusion, f32[32,96]{1,0:T(8,128)S(1)} %broadcast_multiply_fusion, f32[128]{0:T(128)} %param.21, f32[128]{0:T(128)} %param.19, bf16[384,128]{1,0:T(8,128)(2,1)S(1)} %copy-done, ...), kind=kOutput, calls=%fused_computation.15 | convolution fusion | flops 410910720 | bytes 3303936 | tf_op jit(solution)/shard_map/dot_general | solution.py:32
  44.0 1.1 copy.34
  45.1 1.1 copy.37
  46.2 1.1 copy.39
  47.4 1.1 copy.41
  48.5 1.1 copy.43
  49.7 1.1 copy.45
  50.8 1.1 copy.47
  51.9 1.4 exponential_reduce_fusion
  53.4 48.4 %all-reduce.5.cloned.1.call-done = f32[32,7,384]{0,1,2:T(8,128)} async-done(((f32[32,7,384]{0,1,2:T(8,128)}), f32[32,7,384]{0,1,2:T(8,128)}) %all-reduce.5.cloned.1.call-update) | async-done | bytes 344080 | tf_op jit(solution)/shard_map/psum | solution.py:12
  101.7 6.8 %fusion.32 = (f32[32,1,384]{0,1,2:T(1,128)S(1)}, f32[32,1,384]{0,1,2:T(1,128)S(1)}, f32[32,1,384]{0,1,2:T(1,128)S(1)}, f32[32,1,384]{0,1,2:T(1,128)S(1)}, f32[32...) fusion(f32[32,7,384]{0,1,2:T(8,128)} %all-reduce.5.cloned.1.call-done), kind=kLoop, calls=%fused_computation.44 | loop fusion | bytes 688128 | tf_op jit(solution)/shard_map/slice | solution.py:77
  108.5 0.1 copy.35
  108.6 0.1 copy.36
  108.7 0.1 copy.38
  108.8 0.1 copy.40
  108.9 0.1 copy.42
  109.1 0.1 copy.44
  109.2 0.1 copy.46
  109.3 0.0 copy-start.1
  109.3 98.8 %multiply_reduce_fusion = (f32[32,768]{1,0:T(8,128)}, f32[32,768]{1,0:T(8,128)}) fusion(s32[32,384,768]{2,1,0:T(8,128)} %param.12, f32[32,768]{1,0:T(8,128)S(1)} %copy.47, f32[32,384]{1,0:T(8,128)S(1)} %copy.46, f32[32,768]{1,0:T(8,128)S(1)} %copy.45, f32[32,384]{1,0:T(8,128)S(1)} %copy.44, f32[32,768]{1,0:T(8,128)S(1)} %copy.43, f32[32,384]{1,0:T(8,128)S(1)} %copy.42, ...), kind=kLoop, calls=%fused_computation.1 | loop fusion | flops 471810048 | bytes 38977536 | tf_op jit(solution)/shard_map/reduce_sum | solution.py:78
  208.1 0.0 all-reduce.7.cloned.1.call-update
  208.2 53.1 %all-reduce.7.cloned.1.call-done = (f32[32,768]{1,0:T(8,128)}, f32[32,768]{1,0:T(8,128)}) async-done(((f32[32,768]{1,0:T(8,128)}, f32[32,768]{1,0:T(8,128)}), (f32[32,768]{1,0:T(8,128)}, f32[32,768]{1,0:T(8,128)})) %all-reduce.7.cloned.1.call-update) | async-done | bytes 196624 | tf_op jit(solution)/shard_map/psum | solution.py:80
  261.3 0.9 maximum_divide_fusion
  262.1 0.0 copy-start.2
  262.1 0.4 fusion.33
  262.6 0.0 copy-done.1
  262.6 1.3 fusion.30
  263.9 39.6 %all-reduce = (f32[]{:T(128)}, f32[]{:T(128)}) all-reduce(f32[]{:T(128)} %get-tuple-element.12, f32[]{:T(128)} %get-tuple-element.28), channel_id=1, replica_groups=mesh['row'=4,'col'=8] {'row','col'}, use_global_device_ids=true, to_apply=%region_11.12 | all-reduce | flops 2 | bytes 16 | tf_op jit(solution)/shard_map/psum | solution.py:87
  304.7 0.0 copy-done.2
  (3 shorter events, 0.0 us)
Async XLA Ops:
  7.2 33.6 %copy-start = (bf16[384,128]{1,0:T(8,128)(2,1)S(1)}, bf16[384,128]{1,0:T(8,128)(2,1)}, u32[]{:S(2)}) copy-start(bf16[384,128]{1,0:T(8,128)(2,1)} %param.18) | copy-start | bytes 294916
  7.2 94.6 %all-reduce.5.cloned.1.call-start = ((), (), s32[]{:S(2)}) async-start(), calls=%async_computation | async-start | bytes 3145728 | tf_op jit(solution)/shard_map/psum | solution.py:12
  32.3 228.9 %all-reduce.7.cloned.1.call-start = ((), (), s32[]{:S(2)}) async-start(), calls=%async_computation.1 | async-start | bytes 393216 | tf_op jit(solution)/shard_map/psum | solution.py:80
  109.3 153.3 %copy-start.1 = (s32[32,96]{1,0:T(8,128)S(1)}, s32[32,96]{1,0:T(8,128)}, u32[]{:S(2)}) copy-start(s32[32,96]{1,0:T(8,128)} %param.15) | copy-start | bytes 36868
  262.1 42.6 %copy-start.2 = (f32[32,96]{1,0:T(8,128)}, f32[32,96]{1,0:T(8,128)S(1)}, u32[]{:S(2)}) copy-start(f32[32,96]{1,0:T(8,128)S(1)} %maximum_divide_fusion) | copy-start | bytes 36868
Sparse Core Ops, SparseCore 0:
  32.5 69.2 all-reduce.4
  208.3 52.9 all-reduce.6
where the time goes:
time: 314 us; the launch traced here: 313 us
  other arithmetic  109 us (35%)
  waiting for transfers between devices  102 us (32%)
  blocking collectives  60.8 us (19%)
  local copies, waits for them, and re-layouts  19.7 us (6%)
  between operations  16.6 us (5%)
  matrix products  4.59 us (1%)
    reduce_sum x1, other arithmetic, local(): preserved = jnp.sum(weights * scores, axis=1)  98.8 us
    psum x1, waiting for transfers between devices, local(): preserved_all, neighbors_all = lax.psum((preserved, neighbors), 'col')  53.1 us
    psum x1, waiting for transfers between devices, from_root(): return lax.psum(jnp.where(mine, shard, jnp.zeros_like(shard)), axis)  48.4 us
    psum x1, blocking collectives, local(): lax.psum((jnp.sum(residue_loss), jnp.sum(valid)), ('row', 'col'))  39.6 us
    all_gather x1, blocking collectives, local(): rows_part = lax.all_gather(stacked, 'col', axis=2, tiled=True)  21.3 us
    slice x1, local copies, waits for them, and re-layouts, local(): cols_part[:, 6, :, None]  6.78 us
  transfers between devices with their start and end apart: 2, of which 2 were waited for; matrix products, arithmetic and copies ran while one was open for 7% of the time, Pallas kernels for 0%

commit v1 on v0

--- a/solution.py
+++ b/solution.py
@@ -7,9 +7,13 @@
 THRESHOLDS = (0.5, 1.0, 2.0, 4.0)
 
 
+def choose_the_zone(local_block, axis_key):
+    return jnp.sum(lax.all_gather(local_block, axis_name=axis_key), axis=0)
+
+
 def from_root(shard, axis, root):
     mine = lax.axis_index(axis) == root
-    return lax.psum(jnp.where(mine, shard, jnp.zeros_like(shard)), axis)
+    return choose_the_zone(jnp.where(mine, shard, jnp.zeros_like(shard)), axis)
 
 
 def tile_dist(rows_block, cols_block):

time: 314 us -> 276 us (0.88)
  waiting for transfers between devices: 102 us -> 66.1 us
  local copies, waits for them, and re-layouts: 19.7 us -> 16 us
    psum x1 -> x0, waiting for transfers between devices: 48.4 us -> none  [from_root(): return lax.psum(jnp.where(mine, shard, jnp.zeros_like(shard)), axis)]
    all_gather x0 -> x1, waiting for transfers between devices: none -> 13 us  [choose_the_zone(): return jnp.sum(lax.all_gather(local_block, axis_name=axis_key), axis=0)]
    slice x1 -> x0, local copies, waits for them, and re-layouts: 6.78 us -> none  [local(): cols_part[:, 6, :, None]]
  transfers between devices with their start and end apart: 2 -> 2, of which waited for: 2 -> 2; matrix products, arithmetic and copies ran while one was open for 7% -> 8% of each run, Pallas kernels for 0% -> 0%
where the time goes in v1:
time: 276 us; the launch traced here: 275 us
  other arithmetic  111 us (40%)
  waiting for transfers between devices  66.1 us (24%)
  blocking collectives  60.8 us (22%)
  between operations  16.6 us (6%)
  local copies, waits for them, and re-layouts  16 us (6%)
  matrix products  4.6 us (2%)
    reduce_sum x1, other arithmetic, local(): preserved = jnp.sum(weights * scores, axis=1)  98.8 us
    psum x1, waiting for transfers between devices, local(): preserved_all, neighbors_all = lax.psum((preserved, neighbors), 'col')  53 us
    psum x1, blocking collectives, local(): lax.psum((jnp.sum(residue_loss), jnp.sum(valid)), ('row', 'col'))  39.5 us
    all_gather x1, blocking collectives, local(): rows_part = lax.all_gather(stacked, 'col', axis=2, tiled=True)  21.3 us
    all_gather x1, waiting for transfers between devices, choose_the_zone(): return jnp.sum(lax.all_gather(local_block, axis_name=axis_key), axis=0)  13 us
  transfers between devices with their start and end apart: 2, of which 2 were waited for; matrix products, arithmetic and copies ran while one was open for 8% of the time, Pallas kernels for 0%

profile of v1, /device:TPU:0, one launch (start us, length us, event | category | flops | bytes accessed | tf_op | source)
XLA Modules:
  0.0 275.4 jit_solution(11662590257304280294)
XLA Ops:
  7.2 0.0 copy-start
  7.2 0.0 all-gather.3.cloned.1.call-start
  7.3 0.7 convert_bitcast_fusion
  8.0 0.8 pad_maximum_fusion
  8.8 0.9 copy.38
  9.7 21.3 %all_gather.9 = f32[32,7,768]{0,1,2:T(8,128)S(1)} all-gather(f32[32,7,96]{0,1,2:T(8,128)} %copy.38), channel_id=1, replica_groups=mesh['row'=4,'col'=8] {'col'}, dimensions={2}, use_global_device_ids=true | all-gather | bytes 774144 | tf_op jit(solution)/shard_map/all_gather | solution.py:69
  31.0 1.3 constant_dynamic-slice_fusion
  32.3 2.5 copy.47
  34.8 1.7 broadcast_select_fusion
  36.5 0.0 all-gather.3.cloned.1.call-update
  36.6 0.0 all-reduce.4.cloned.1.call-start
  36.6 3.3 %fusion.31 = (f32[32,1,768]{0,1,2:T(1,128)}, f32[32,1,768]{0,1,2:T(1,128)}, f32[32,1,768]{0,1,2:T(1,128)}, f32[32,1,768]{0,1,2:T(1,128)}, f32[32,1,768]{0,1,2:T(...) fusion(f32[32,7,768]{0,1,2:T(8,128)S(1)} %all_gather.9), kind=kLoop, calls=%fused_computation.51 | loop fusion | bytes 1376256 | tf_op jit(solution)/shard_map/slice | solution.py:81
  39.9 1.1 copy.39
  41.0 1.1 copy.41
  42.1 1.1 copy.42
  43.3 1.2 copy.43
  44.4 1.1 copy.44
  45.6 1.1 copy.45
  46.7 1.1 copy.46
  47.9 2.3 convert_reduce_fusion
  50.2 2.8 %fusion.4 = f32[32,96]{1,0:T(8,128)S(1)} fusion(bf16[32,96,384]{2,1,0:T(8,128)(2,1)} %param.16, f32[32,96]{1,0:T(8,128)S(1)} %broadcast_multiply_fusion), kind=kLoop, calls=%fused_computation.8 | loop fusion | flops 4715520 | bytes 2383872 | tf_op jit(solution)/shard_map/reduce_sum | solution.py:30
  53.0 0.0 copy-done
  53.0 3.2 %maximum_convert_fusion = bf16[32,96,128]{2,1,0:T(8,128)(2,1)S(1)} fusion(bf16[32,96,384]{2,1,0:T(8,128)(2,1)} %param.16, f32[384]{0:T(512)} %param.17, f32[32,96]{1,0:T(8,128)S(1)} %add_rsqrt_fusion, f32[32,96]{1,0:T(8,128)S(1)} %broadcast_multiply_fusion, f32[128]{0:T(128)} %param.21, f32[128]{0:T(128)} %param.19, bf16[384,128]{1,0:T(8,128)(2,1)S(1)} %copy-done, ...), kind=kOutput, calls=%fused_computation.15 | convolution fusion | flops 410910720 | bytes 3303936 | tf_op jit(solution)/shard_map/dot_general | solution.py:36
  56.2 1.4 exponential_reduce_fusion
  57.6 13.0 %all-gather.3.cloned.1.call-done = f32[128,7,384]{2,0,1:T(8,128)} async-done(((f32[32,7,384]{2,0,1:T(8,128)}), f32[128,7,384]{2,0,1:T(8,128)}) %all-gather.3.cloned.1.call-update) | async-done | bytes 1376272 | tf_op jit(solution)/shard_map/all_gather | solution.py:11
  70.6 1.5 reduce_sum.90
  72.1 0.0 copy-start.1
  72.2 98.8 %multiply_reduce_fusion = (f32[32,768]{1,0:T(8,128)}, f32[32,768]{1,0:T(8,128)}) fusion(s32[32,384,768]{2,1,0:T(8,128)} %param.12, f32[32,768]{1,0:T(8,128)S(1)} %copy.46, f32[32,384]{1,0:T(8,128)S(1)} %get-tuple-element.25, f32[32,768]{1,0:T(8,128)S(1)} %copy.45, f32[32,384]{1,0:T(8,128)S(1)} %get-tuple-element.26, f32[32,768]{1,0:T(8,128)S(1)} %copy.44, ...), kind=kLoop, calls=%fused_computation.1 | loop fusion | flops 471810048 | bytes 38977536 | tf_op jit(solution)/shard_map/reduce_sum | solution.py:82
  171.0 0.0 all-reduce.4.cloned.1.call-update
  171.0 53.0 %all-reduce.4.cloned.1.call-done = (f32[32,768]{1,0:T(8,128)}, f32[32,768]{1,0:T(8,128)}) async-done(((f32[32,768]{1,0:T(8,128)}, f32[32,768]{1,0:T(8,128)}), (f32[32,768]{1,0:T(8,128)}, f32[32,768]{1,0:T(8,128)})) %all-reduce.4.cloned.1.call-update) | async-done | bytes 196624 | tf_op jit(solution)/shard_map/psum | solution.py:84
  224.0 0.9 maximum_divide_fusion
  224.9 0.0 copy-start.2
  224.9 0.4 fusion.32
  225.4 0.0 copy-done.1
  225.4 1.3 fusion.30
  226.7 39.5 %all-reduce = (f32[]{:T(128)}, f32[]{:T(128)}) all-reduce(f32[]{:T(128)} %get-tuple-element.15, f32[]{:T(128)} %get-tuple-element.31), channel_id=1, replica_groups=mesh['row'=4,'col'=8] {'row','col'}, use_global_device_ids=true, to_apply=%region_11.12 | all-reduce | flops 2 | bytes 16 | tf_op jit(solution)/shard_map/psum | solution.py:91
  267.5 0.0 copy-done.2
  (4 shorter events, 0.0 us)
Async XLA Ops:
  7.2 45.8 %copy-start = (bf16[384,128]{1,0:T(8,128)(2,1)S(1)}, bf16[384,128]{1,0:T(8,128)(2,1)}, u32[]{:S(2)}) copy-start(bf16[384,128]{1,0:T(8,128)(2,1)} %param.18) | copy-start | bytes 294916
  7.2 63.5 %all-gather.3.cloned.1.call-start = ((), (), s32[]{:S(2)}) async-start(), calls=%async_computation | async-start | bytes 1720320 | tf_op jit(solution)/shard_map/all_gather | solution.py:11
  36.6 187.5 %all-reduce.4.cloned.1.call-start = ((), (), s32[]{:S(2)}) async-start(), calls=%async_computation.1 | async-start | bytes 393216 | tf_op jit(solution)/shard_map/psum | solution.py:84
  72.1 153.2 %copy-start.1 = (s32[32,96]{1,0:T(8,128)S(1)}, s32[32,96]{1,0:T(8,128)}, u32[]{:S(2)}) copy-start(s32[32,96]{1,0:T(8,128)} %param.15) | copy-start | bytes 36868
  224.9 42.6 %copy-start.2 = (f32[32,96]{1,0:T(8,128)}, f32[32,96]{1,0:T(8,128)S(1)}, u32[]{:S(2)}) copy-start(f32[32,96]{1,0:T(8,128)S(1)} %maximum_divide_fusion) | copy-start | bytes 36868
Sparse Core Ops, SparseCore 0:
  36.7 33.9 all-gather.2
  171.1 52.8 all-reduce.3
